TPU v7x, 768 devices: a whole 4x8x12 slice. The times are simulated.
768 devices in a mesh: dp: 96 (over x, z, y_lo), mp: 8 (over y_hi, core).
Axes of the slice: x: 4, y: 8 (y_hi: 4, y_lo: 2; y = y_hi * 2 + y_lo), z: 12, core: 2. Of those that a mesh axis runs over, the one named last changes fastest.
Arguments:
- q_latent: bfloat16 [24576, 2, 768], P('dp', None, 'mp'), may hold values from -6 to 6
- kv_latent: bfloat16 [24576, 2, 256], P('dp', None, 'mp'), may hold values from -6 to 6
- q_head_grad: bfloat16 [24576, 6144], P('dp'), may hold values from -0.125 to 0.125
- k_head_grad: bfloat16 [24576, 6144], P('dp'), may hold values from -0.125 to 0.125
- q_heads: bfloat16 [24576, 6144], P('dp', 'mp'), may hold values from -6 to 6
- k_heads: bfloat16 [24576, 6144], P('dp', 'mp'), may hold values from -6 to 6
- query_pick: int32 [96, 16, 48], P('dp', None, 'mp'), may hold values from 0 to 255
- key_pick: int32 [96, 16, 48], P('dp', None, 'mp'), may hold values from 0 to 255
- q_weight: float32 [96, 768, 128], P('dp', 'mp'), may hold values from -6 to 6
- k_weight: float32 [96, 256, 128], P('dp', 'mp'), may hold values from -6 to 6
- q_moment: float32 [96, 768, 128], P('dp', 'mp'), may hold values from -6 to 6
- k_moment: float32 [96, 256, 128], P('dp', 'mp'), may hold values from -6 to 6
Outputs:
- q_weight_new: float32 [96, 768, 128], P('dp', 'mp')
- k_weight_new: float32 [96, 256, 128], P('dp', 'mp')
- q_moment_new: float32 [96, 768, 128], P('dp', 'mp')
- k_moment_new: float32 [96, 256, 128], P('dp', 'mp')
Inputs may be any that keep to these rules, and one draw needn't show every extreme that they name: `query_pick`: the index of a token among the 256 tokens of its own block b. `key_pick`: the index of a token among the 256 tokens of its own block b.
All inputs are finite; a program needn't handle non-finite values.
Results may differ from a plain program's by a relative error of at most 0.0003.
Values sent between devices are 32-bit elements; how exact they have to be, the bound alone decides.
A program may use at most 64 MiB of HBM per device.

v0:
```python
import math

import jax
import jax.numpy as jnp
from jax import lax
from jax.sharding import Mesh
from jax.sharding import PartitionSpec as P

QR = 1536
KR = 512
ITERS = 5
DP = ("dp_0", "dp_1", "dp_2")
MP = ("mp_0", "mp_1")
DP_MP = ("dp_0", "dp_1", "dp_2", "mp_0", "mp_1")


MOMENTUM = 0.95
STEP_SIZE = 1.0
DECAY = 0.1
CLIP_LEVEL = 0.1
SCORE_SCALE = 1.0 / math.sqrt(192.0)
COEFF_A = 3.4445
COEFF_B = -4.775
COEFF_C = 2.0315
HIGHEST = lax.Precision.HIGHEST


def own_rows(subtotal, axes):
    for axis in axes:
        subtotal = lax.psum_scatter(subtotal, axis, scatter_dimension=0, tiled=True)
    return subtotal


def over_axes(value, axes):
    for axis in axes:
        value = lax.pmax(value, axis)
    return value


def laid_out(parts, dim):
    lengths = list(parts.shape[1:])
    lengths[dim] *= parts.shape[0]
    return jnp.moveaxis(parts, 0, dim).reshape(lengths)


def gather_together(arrays, axis, dims):
    vector = jnp.concatenate([a.reshape(-1) for a in arrays])
    lines, at, finished = (lax.all_gather(vector, axis), 0, [])
    for a, dim in zip(arrays, dims):
        parts = lines[:, at : at + a.size].reshape(-1, *a.shape)
        finished.append(laid_out(parts, dim))
        at += a.size
    return tuple(finished)


def from_behind(value, axis, steps):
    count = lax.axis_size(axis)
    pairs = [(source, (source + steps) % count) for source in range(count)]
    return lax.ppermute(value, axis, pairs)


def gramian(matrix):
    return jnp.einsum("rc,rd->cd", matrix, matrix, precision=HIGHEST)


def unchanged(stacked):
    return stacked


def polar_steps(q_rows_in, k_rows_in, combine):
    grams = combine(jnp.stack([gramian(q_rows_in), gramian(k_rows_in)]))
    scale = 1.0 / jnp.sqrt(jnp.trace(grams, axis1=1, axis2=2) + 1.0)
    current = [q_rows_in * scale[0], k_rows_in * scale[1]]
    grams = grams * (scale * scale)[:, None, None]
    for step in range(ITERS):
        updated = []
        for member in range(2):
            square = jnp.dot(grams[member], grams[member], precision=HIGHEST)
            mixer = COEFF_B * grams[member] + COEFF_C * square
            updated.append(
                COEFF_A * current[member] + jnp.dot(current[member], mixer, precision=HIGHEST)
            )
        current = updated
        if step + 1 < ITERS:
            grams = combine(jnp.stack([gramian(current[0]), gramian(current[1])]))
    return (current[0], current[1])


def local(
    q_latent,
    kv_latent,
    q_head_grad,
    k_head_grad,
    q_heads,
    k_heads,
    query_pick,
    key_pick,
    q_weight,
    k_weight,
    q_moment,
    k_moment,
):
    head_count = lax.axis_size(DP) // 2
    tokens_here = q_latent.shape[0]
    q_rows = q_latent.shape[2]
    k_rows = kv_latent.shape[2]
    row_count = q_rows + k_rows
    width = q_moment.shape[2]
    q_grads = q_head_grad.reshape(tokens_here, head_count, width)
    k_grads = k_head_grad.reshape(tokens_here, head_count, width)
    slot_count = row_count * lax.axis_size(DP) // row_count
    slot_ids = jnp.arange(slot_count, dtype=jnp.int32)
    halves = slot_ids // head_count
    owners = slot_ids % head_count
    q_side = jnp.take(q_latent, halves, axis=1)
    k_side = jnp.take(kv_latent, halves, axis=1)
    q_cols = jnp.take(q_grads, owners, axis=1)
    k_cols = jnp.take(k_grads, owners, axis=1)
    q_term = jnp.einsum("tnr,tnc->nrc", q_side, q_cols, preferred_element_type=jnp.float32)
    k_term = jnp.einsum("tnr,tnc->nrc", k_side, k_cols, preferred_element_type=jnp.float32)
    own_term = own_rows(
        jnp.concatenate([q_term, k_term], axis=1).reshape(row_count * lax.axis_size(DP), width), DP
    )
    q_moment_new = MOMENTUM * q_moment[0] + own_term[:q_rows]
    k_moment_new = MOMENTUM * k_moment[0] + own_term[q_rows:]
    local_heads = query_pick.shape[2]
    q_cube = q_heads.reshape(tokens_here, local_heads, width)
    k_cube = k_heads.reshape(tokens_here, local_heads, width)
    picked_q = jnp.take_along_axis(q_cube, query_pick[0][:, :, None], axis=0)
    picked_k = jnp.take_along_axis(k_cube, key_pick[0][:, :, None], axis=0)
    scores = (
        jnp.sum(picked_q.astype(jnp.float32) * picked_k.astype(jnp.float32), axis=2) * SCORE_SCALE
    )
    local_peak = jnp.max(scores, axis=0)
    filled = jnp.full((head_count,), -1e30, jnp.float32)
    filled = lax.dynamic_update_slice(filled, local_peak, (lax.axis_index(MP) * local_heads,))
    peaks = over_axes(filled, DP_MP)
    own_head = lax.axis_index(DP) % head_count
    peak = lax.dynamic_index_in_dim(peaks, own_head, keepdims=False)
    shrink = jnp.sqrt(CLIP_LEVEL / jnp.maximum(peak, CLIP_LEVEL))
    q_half, k_half = gather_together((q_moment_new, k_moment_new), MP, (0, 0))
    place = lax.axis_index(MP)
    q_len = q_half.shape[0]
    k_len = k_half.shape[0]
    joined = jnp.concatenate([q_half, k_half], axis=0)
    other = from_behind(joined, DP, lax.axis_size(DP) // 2)
    q_other = other[:q_len]
    k_other = other[q_len:]
    first = lax.axis_index(DP) < head_count
    q_full = jnp.concatenate(
        [jnp.where(first, q_half, q_other), jnp.where(first, q_other, q_half)], axis=0
    )
    k_full = jnp.concatenate(
        [jnp.where(first, k_half, k_other), jnp.where(first, k_other, k_half)], axis=0
    )
    q_whole, k_whole = polar_steps(q_full, k_full, unchanged)
    second = jnp.where(first, 0, 1).astype(jnp.int32)
    q_ortho = lax.dynamic_slice_in_dim(q_whole, second * q_len + place * q_rows, q_rows, 0)
    k_ortho = lax.dynamic_slice_in_dim(k_whole, second * k_len + place * k_rows, k_rows, 0)
    keep = 1.0 - STEP_SIZE * DECAY
    q_weight_new = (q_weight[0] * keep - STEP_SIZE * 0.2 * math.sqrt(QR) * q_ortho) * shrink
    k_weight_new = (k_weight[0] * keep - STEP_SIZE * 0.2 * math.sqrt(KR) * k_ortho) * shrink
    return (q_weight_new[None], k_weight_new[None], q_moment_new[None], k_moment_new[None])


def solution(mesh):
    split = Mesh(mesh.devices.reshape(4, 12, 2, 4, 2), ("dp_0", "dp_1", "dp_2", "mp_0", "mp_1"))
    placed = (
        P(DP, None, MP),
        P(DP, None, MP),
        P(DP, None),
        P(DP, None),
        P(DP, MP),
        P(DP, MP),
        P(DP, None, MP),
        P(DP, None, MP),
        P(DP, MP, None),
        P(DP, MP, None),
        P(DP, MP, None),
        P(DP, MP, None),
    )
    return jax.shard_map(
        local,
        mesh=split,
        in_specs=placed,
        out_specs=(P(DP, MP, None), P(DP, MP, None), P(DP, MP, None), P(DP, MP, None)),
        check_vma=False,
    )
```

profile of v0, /device:TPU:1, one launch (start us, length us, event | category | flops | bytes accessed | tf_op | source)
XLA Modules:
  0.0 332.5 jit_solution(8802076614212059209)
XLA Ops:
  7.3 4.6 %copy.77 = bf16[256,6144]{0,1:T(8,128)(2,1)} copy(bf16[256,6144]{1,0:T(8,128)(2,1)} %param.18) | data formatting | bytes 6291456 | tf_op args[2]
  11.9 3.5 %copy.78 = bf16[256,48,128]{2,0,1:T(8,128)(2,1)S(1)} copy(bf16[256,48,128]{0,2,1:T(8,128)(2,1)} %bitcast.135) | data formatting | bytes 6291456 | tf_op jit(solution)/shard_map/reshape | solution.py:109
  15.4 4.6 %copy.79 = bf16[256,6144]{0,1:T(8,128)(2,1)} copy(bf16[256,6144]{1,0:T(8,128)(2,1)} %param.19) | data formatting | bytes 6291456 | tf_op args[3]
  20.1 4.7 %copy.80 = bf16[256,48,128]{2,0,1:T(8,128)(2,1)} copy(bf16[256,48,128]{0,2,1:T(8,128)(2,1)} %bitcast.136) | data formatting | bytes 6291456 | tf_op jit(solution)/shard_map/reshape | solution.py:110
  24.8 6.0 %gather_fusion.2 = bf16[96,256,128]{2,1,0:T(8,128)(2,1)} fusion(bf16[256,48,128]{2,0,1:T(8,128)(2,1)S(1)} %copy.78, s32[1024]{0:T(1024)S(1)} %pad_clamp_fusion), kind=kCustom, calls=%fused_computation.clone | custom fusion | bytes 12583296 | tf_op jit(solution)/shard_map/jit(_take)/gather | solution.py:117
  30.8 7.9 %gather_fusion.3 = bf16[96,256,128]{2,1,0:T(8,128)(2,1)} fusion(bf16[256,48,128]{2,0,1:T(8,128)(2,1)} %copy.80, s32[1024]{0:T(1024)S(1)} %pad_clamp_fusion), kind=kCustom, calls=%fused_computation.2.clone | custom fusion | bytes 12583296 | tf_op jit(solution)/shard_map/jit(_take)/gather | solution.py:118
  38.7 3.1 gather_fusion
  41.8 0.7 gather_fusion.1
  42.5 5.7 %fusion.2 = f32[96,96,128]{2,1,0:T(8,128)S(1)} fusion(bf16[96,256,128]{2,1,0:T(8,128)(2,1)} %gather_fusion.2, pred[96]{0:T(512)(128)(4,1)S(1)} %get-tuple-element.18, bf16[96,256,96]{1,2,0:T(8,128)(2,1)} %gather_fusion, pred[96]{0:T(512)(128)(4,1)S(1)} %get-tuple-element.19), kind=kOutput, calls=%fused_computation.9 | convolution fusion | flops 609484800 | bytes 15728832 | tf_op jit(solution)/shard_map/tnr,tnc->nrc/dot_general | solution.py:119
  48.3 3.5 %fusion = f32[96,32,128]{2,1,0:T(8,128)S(1)} fusion(bf16[96,256,128]{2,1,0:T(8,128)(2,1)} %gather_fusion.3, pred[96]{0:T(512)(128)(4,1)S(1)} %get-tuple-element.18, bf16[96,256,32]{1,2,0:T(8,128)(2,1)S(1)} %gather_fusion.1, pred[96]{0:T(512)(128)(4,1)S(1)} %get-tuple-element.19), kind=kOutput, calls=%fused_computation.7 | convolution fusion | flops 205258752 | bytes 9437376 | tf_op jit(solution)/shard_map/tnr,tnc->nrc/dot_general | solution.py:120
  51.8 3.2 pad_maximum_fusion
  55.2 79.6 %reduce-scatter.4.cloned.1.call-done = f32[3072,128]{1,0:T(8,128)} async-done(((f32[12288,128]{1,0:T(8,128)}), f32[3072,128]{1,0:T(8,128)}) %reduce-scatter.4.cloned.1.call-update) | async-done | bytes 1572880 | tf_op jit(solution)/shard_map/reduce_scatter | solution.py:30
  134.9 55.9 %reduce-scatter.6.cloned.1.call-done = f32[256,128]{1,0:T(8,128)} async-done(((f32[3072,128]{1,0:T(8,128)}), f32[256,128]{1,0:T(8,128)}) %reduce-scatter.6.cloned.1.call-update) | async-done | bytes 131088 | tf_op jit(solution)/shard_map/reduce_scatter | solution.py:30
  190.9 0.2 copy.82
  191.1 0.2 copy.84
  191.5 1.5 gather_fusion.4
  193.2 0.2 copy.88
  193.6 1.5 gather_fusion.5
  195.3 24.7 %reduce-scatter.8.cloned.1.call-done = f32[128,128]{1,0:T(8,128)} async-done(((f32[256,128]{1,0:T(8,128)}), f32[128,128]{1,0:T(8,128)}) %reduce-scatter.8.cloned.1.call-update) | async-done | bytes 65552 | tf_op jit(solution)/shard_map/reduce_scatter | solution.py:30
  220.0 1.4 fusion.41
  221.4 1.3 fusion.43
  222.7 17.2 %all-gather = f32[131072]{0:T(1024)S(1)} all-gather(f32[16384]{0:T(1024)S(1)} %pad_maximum_fusion.9), channel_id=2, replica_groups=mesh['dp_0'=4,'dp_1'=12,'dp_2'=2,'mp_0'=4,'mp_1'=2] {'mp_0','mp_1'}, dimensions={0}, use_global_device_ids=true | all-gather | bytes 589824 | tf_op jit(solution)/shard_map/all_gather | solution.py:48
  240.3 4.6 %collective-permute-start = (f32[1024,128]{1,0:T(8,128)S(1)}, f32[1024,128]{1,0:T(8,128)S(1)}, u32[]{:S(2)}, u32[]{:S(2)}) collective-permute-start(f32[1024,128]{1,0:T(8,128)S(1)} %pad_maximum_fusion.4), channel_id=1, source_target_pairs={{0,384},{8,392},{16,400},{24,408},{32,416},{40,424},{48,432},{56,4... | collective-permute-start | bytes 1572872 | tf_op jit(solution)/shard_map/ppermute | solution.py:59
  245.1 0.2 multiply_reduce_fusion
  245.5 0.2 dynamic_update_slice.3
  245.7 12.7 %pmax.35 = f32[48]{0:T(128)S(1)} all-reduce(f32[48]{0:T(128)S(1)} %dynamic_update_slice.3), channel_id=1, replica_groups=mesh['dp_0'=4,'dp_1'=12,'dp_2'=2,'mp_0'=4,'mp_1'=2] {'dp_0'}, use_global_device_ids=true, to_apply=%region_6.9 | all-reduce | flops 48 | bytes 384 | tf_op jit(solution)/shard_map/pmax | solution.py:36
  258.4 19.8 %pmax.36 = f32[48]{0:T(128)S(1)} all-reduce(f32[48]{0:T(128)S(1)} %pmax.35), channel_id=1, replica_groups=mesh['dp_0'=4,'dp_1'=12,'dp_2'=2,'mp_0'=4,'mp_1'=2] {'dp_1'}, use_global_device_ids=true, to_apply=%region_7.10 | all-reduce | flops 48 | bytes 384 | tf_op jit(solution)/shard_map/pmax | solution.py:36
  278.2 3.9 %pmax.37 = f32[48]{0:T(128)S(1)} all-reduce(f32[48]{0:T(128)S(1)} %pmax.36), channel_id=1, replica_groups=mesh['dp_0'=4,'dp_1'=12,'dp_2'=2,'mp_0'=4,'mp_1'=2] {'dp_2'}, use_global_device_ids=true, to_apply=%region_8.11 | all-reduce | flops 48 | bytes 384 | tf_op jit(solution)/shard_map/pmax | solution.py:36
  282.1 8.3 %pmax.38 = f32[48]{0:T(128)S(1)} all-reduce(f32[48]{0:T(128)S(1)} %pmax.37), channel_id=1, replica_groups=mesh['dp_0'=4,'dp_1'=12,'dp_2'=2,'mp_0'=4,'mp_1'=2] {'mp_0'}, use_global_device_ids=true, to_apply=%region_9.12 | all-reduce | flops 48 | bytes 384 | tf_op jit(solution)/shard_map/pmax | solution.py:36
  290.4 12.5 %pmax.39 = f32[48]{0:T(128)S(1)} all-reduce(f32[48]{0:T(128)S(1)} %pmax.38), channel_id=1, replica_groups=mesh['dp_0'=4,'dp_1'=12,'dp_2'=2,'mp_0'=4,'mp_1'=2] {'mp_1'}, use_global_device_ids=true, to_apply=%region_10.13 | all-reduce | flops 48 | bytes 384 | tf_op jit(solution)/shard_map/pmax | solution.py:36
  302.9 0.6 dynamic_slice.11
  304.3 1.4 convolution_bitcast_fusion
  305.8 0.6 convolution_bitcast_fusion.1
  306.6 0.2 fusion.21
  306.8 0.2 fusion.26
  307.0 0.6 fusion.53
  307.6 1.0 convolution_add_fusion.7
  308.6 0.6 fusion.59
  309.2 0.2 fusion.20
  309.4 0.4 convolution_add_fusion.6
  309.8 0.6 fusion.60
  310.4 0.2 fusion.19
  310.6 0.4 convolution_add_fusion.5
  311.0 0.6 fusion.61
  311.6 0.2 fusion.18
  311.8 0.4 convolution_add_fusion.4
  312.2 0.6 fusion.62
  312.8 0.2 fusion.17
  313.0 0.4 fusion.63
  313.4 1.4 convolution_add_fusion.3
  314.8 1.4 fusion.54
  316.2 0.2 fusion.25
  316.4 0.8 convolution_add_fusion.2
  317.2 1.4 fusion.55
  318.6 0.2 fusion.24
  318.8 1.0 convolution_add_fusion.1
  319.9 1.4 fusion.56
  321.3 0.2 fusion.23
  321.5 0.8 convolution_add_fusion
  322.3 1.4 fusion.57
  323.7 0.2 fusion.22
  323.9 0.8 fusion.58
  324.7 0.6 fusion.40
  325.3 0.6 fusion.36
  (61 shorter events, 1.8 us)
Async XLA Ops:
  7.2 31.5 %copy-start = (bf16[256,2,96]{0,2,1:T(8,128)(2,1)S(1)}, bf16[256,2,96]{0,2,1:T(8,128)(2,1)}, u32[]{:S(2)}) copy-start(bf16[256,2,96]{0,2,1:T(8,128)(2,1)} %param.16) | copy-start | bytes 294916
  7.2 127.6 %reduce-scatter.4.cloned.1.call-start = ((), (), s32[]{:S(2)}) async-start(), calls=%async_computation.3 | async-start | bytes 7864320 | tf_op jit(solution)/shard_map/reduce_scatter | solution.py:30
  38.7 3.2 copy-start.1
  55.0 79.8 %copy-start.8 = (s32[1,16,6]{1,0,2:T(1,128)S(1)}, s32[1,16,6]{1,0,2:T(1,128)}, u32[]{:S(2)}) copy-start(s32[1,16,6]{1,0,2:T(1,128)} %param.22) | copy-start | bytes 1156
  55.0 135.8 %copy-start.9 = (s32[1,16,6]{1,0,2:T(1,128)S(1)}, s32[1,16,6]{1,0,2:T(1,128)}, u32[]{:S(2)}) copy-start(s32[1,16,6]{1,0,2:T(1,128)} %param.23) | copy-start | bytes 1156
  55.0 135.8 %copy-start.2 = (bf16[256,768]{1,0:T(8,128)(2,1)S(1)}, bf16[256,768]{1,0:T(8,128)(2,1)}, u32[]{:S(2)}) copy-start(bf16[256,768]{1,0:T(8,128)(2,1)} %param.20) | copy-start | bytes 1179652
  55.0 138.0 %copy-start.3 = (bf16[256,768]{1,0:T(8,128)(2,1)S(1)}, bf16[256,768]{1,0:T(8,128)(2,1)}, u32[]{:S(2)}) copy-start(bf16[256,768]{1,0:T(8,128)(2,1)} %param.21) | copy-start | bytes 1179652
  55.1 164.9 %copy-start.4 = (f32[1,96,128]{2,1,0:T(8,128)S(1)}, f32[1,96,128]{2,1,0:T(8,128)}, u32[]{:S(2)}) copy-start(f32[1,96,128]{2,1,0:T(8,128)} %param.26) | copy-start | bytes 147460
  55.1 166.3 %copy-start.6 = (f32[1,32,128]{2,1,0:T(8,128)S(1)}, f32[1,32,128]{2,1,0:T(8,128)}, u32[]{:S(2)}) copy-start(f32[1,32,128]{2,1,0:T(8,128)} %param.27) | copy-start | bytes 49156
  55.1 135.7 %reduce-scatter.6.cloned.1.call-start = ((), (), s32[]{:S(2)}) async-start(), calls=%async_computation.4 | async-start | bytes 1703936 | tf_op jit(solution)/shard_map/reduce_scatter | solution.py:30
  134.8 85.2 %reduce-scatter.8.cloned.1.call-start = ((), (), s32[]{:S(2)}) async-start(), calls=%async_computation.5 | async-start | bytes 196608 | tf_op jit(solution)/shard_map/reduce_scatter | solution.py:30
  240.3 64.0 %collective-permute-start = (f32[1024,128]{1,0:T(8,128)S(1)}, f32[1024,128]{1,0:T(8,128)S(1)}, u32[]{:S(2)}, u32[]{:S(2)}) collective-permute-start(f32[1024,128]{1,0:T(8,128)S(1)} %pad_maximum_fusion.4), channel_id=1, source_target_pairs={{0,384},{8,392},{16,400},{24,408},{32,416},{40,424},{48,432},{56,4... | collective-permute-start | bytes 1572872 | tf_op jit(solution)/shard_map/ppermute | solution.py:59
  318.6 6.1 %copy-start.7 = (f32[1,32,128]{2,1,0:T(8,128)S(1)}, f32[1,32,128]{2,1,0:T(8,128)}, u32[]{:S(2)}) copy-start(f32[1,32,128]{2,1,0:T(8,128)} %param.25) | copy-start | bytes 49156
  318.6 6.7 %copy-start.5 = (f32[1,96,128]{2,1,0:T(8,128)S(1)}, f32[1,96,128]{2,1,0:T(8,128)}, u32[]{:S(2)}) copy-start(f32[1,96,128]{2,1,0:T(8,128)} %param.24) | copy-start | bytes 147460
Sparse Core Ops, SparseCore 0:
  55.2 79.5 reduce-scatter.3
  137.9 52.8 reduce-scatter.5
  193.9 26.0 reduce-scatter.7
where the time goes:
time: 333 us; the launch traced here: 332 us
  waiting for transfers between devices  160 us (48%)
  blocking collectives  74.4 us (22%)
  local copies, waits for them, and re-layouts  41.4 us (12%)
  matrix products  28.5 us (9%)
  between operations  15.1 us (5%)
  other arithmetic  7.99 us (2%)
  starting transfers between devices  4.76 us (1%)
    reduce_scatter x3, waiting for transfers between devices, own_rows(): subtotal = lax.psum_scatter(subtotal, axis, scatter_dimension=0, tiled=True)  160 us
    pmax x5, blocking collectives, over_axes(): value = lax.pmax(value, axis)  57.2 us
    all_gather x1, blocking collectives, gather_together(): lines, at, finished = (lax.all_gather(vector, axis), 0, [])  17.2 us
    dot_general x10, matrix products, gramian(): return jnp.einsum('rc,rd->cd', matrix, matrix, precision=HIGHEST)  10.1 us
    unnamed x24, local copies, waits for them, and re-layouts  9.69 us
    gather x1, local copies, waits for them, and re-layouts, local(): k_cols = jnp.take(k_grads, owners, axis=1)  7.9 us
    dot_general x10, matrix products, polar_steps(): jnp.dot(current[member], mixer, precision=HIGHEST)  7.17 us
  transfers between devices with their start and end apart: 4, of which 3 were waited for; matrix products, arithmetic and copies ran while one was open for 2% of the time, Pallas kernels for 0%

commit v1 on v0

v1 whole, which is shorter than its diff:
```python
import functools
import heapq
import math

import jax
import jax.numpy as jnp
from jax import lax
from jax.experimental import pallas as pl
from jax.experimental.pallas import tpu as pltpu
from jax.sharding import Mesh
from jax.sharding import PartitionSpec as P

QR = 1536
KR = 512
ITERS = 5
AXES = ("dp_0", "dp_1", "dp_2", "mp_0", "mp_1")
DP = AXES[:3]
MP = AXES[3:]
SHAPE = (4, 12, 2, 4, 2)

MOMENTUM = 0.95
STEP_SIZE = 1.0
DECAY = 0.1
CLIP_LEVEL = 0.1
SCORE_SCALE = 1.0 / math.sqrt(192.0)
COEFF_A = 3.4445
COEFF_B = -4.775
COEFF_C = 2.0315
LOWEST = -1e30
W = 128
PEAK_ROWS = 8


def chains(n, parity):
    far, near = n // 2, n - 1 - n // 2
    return {-1: far, 1: near} if parity == 0 else {-1: near, 1: far}


def message_bytes(stream, stage, sizes):
    size = stream["rows"] * W * 4
    if not stream["peak"]:
        for axis in stream["order"][stage + 1 :]:
            size *= sizes[axis]
    return size


def plan(streams, sizes, rate=46.6e3, latency=2.4, backlog=8.0, turn=0.15):
    free, pool, acts, events, left = {}, [], [], [], {}
    count = 0

    def start_stage(i, k):
        stream = streams[i]
        lengths = chains(sizes[stream["order"][k]], stream["parity"])
        left[i, k] = sum(length > 0 for length in lengths.values())
        for way, length in lengths.items():
            if length > 0:
                pool.append(((-k if k else 1, -length if k == 0 else 0, i), (i, k, way, 0)))

    def fill(now):
        nonlocal count
        pool.sort()
        kept = []
        for item in pool:
            i, k, way, _ = item[1]
            axis = streams[i]["order"][k]
            link = (axis, way if sizes[axis] > 2 else 0)
            if free.get(link, 0.0) - now < backlog:
                begin = max(free.get(link, 0.0), now)
                free[link] = begin + message_bytes(streams[i], k, sizes) / rate
                count += 1
                heapq.heappush(events, (free[link] + latency, count, item[1]))
                acts.append(("send",) + item[1])
            else:
                kept.append(item)
        pool[:] = kept

    now = 0.0
    for i in range(len(streams)):
        start_stage(i, 0)
    fill(now)
    while events:
        at, _, (i, k, way, t) = heapq.heappop(events)
        now = max(now, at) + turn
        stream = streams[i]
        length = chains(sizes[stream["order"][k]], stream["parity"])[way]
        acts.append(("recv", i, k, way, t))
        if t < length - 1:
            pool.append(((-k if k else 0, -(length - t), i), (i, k, way, t + 1)))
        else:
            left[i, k] -= 1
            if left[i, k] == 0:
                acts.append(("close", i, k))
                if k < 2:
                    start_stage(i, k + 1)
        fill(now)
    return acts


def make_streams(q_rows, k_rows):
    piece = q_rows // 6
    streams = [dict(peak=True, rows=PEAK_ROWS, order=(0, 2, 1), parity=0)]
    for n in range(4):
        streams.append(
            dict(peak=False, kind=0, at=n * piece, rows=piece, order=(0, 2, 1), parity=n % 2)
        )
    for n in range(4, 6):
        streams.append(
            dict(peak=False, kind=0, at=n * piece, rows=piece, order=(1, 0, 2), parity=n % 2)
        )
    for n in range(2):
        streams.append(
            dict(
                peak=False,
                kind=1,
                at=n * (k_rows // 2),
                rows=k_rows // 2,
                order=(1, 0, 2),
                parity=n % 2,
            )
        )
    return streams


def split(x):
    high = x.astype(jnp.bfloat16)
    low = (x - high.astype(jnp.float32)).astype(jnp.bfloat16)
    return jnp.concatenate([high, low], axis=1)


def contract_rows(a, b):
    return lax.dot_general(a, b, (((0,), (0,)), ((), ())), preferred_element_type=jnp.float32)


def gramian(pair):
    g = contract_rows(pair, pair)
    return (g[:W, :W] + g[W:, W:]) + (g[:W, W:] + g[W:, :W])


def mixer_of(gram):
    square = jnp.dot(
        gram, gram, precision=lax.Precision.HIGHEST, preferred_element_type=jnp.float32
    )
    mixer = split(COEFF_B * gram + COEFF_C * square)
    return jnp.concatenate([mixer, mixer], axis=0)


def mixed(pair, mixer):
    out = jnp.dot(pair, mixer, preferred_element_type=jnp.float32)
    return out[:, :W] + out[:, W:]


def body(
    sizes,
    q_rows,
    k_rows,
    picks,
    tokens,
    local_heads,
    streams,
    acts,
    q_lat,
    k_lat,
    q_grad_hbm,
    k_grad_hbm,
    q_heads,
    k_heads,
    q_pick,
    k_pick,
    q_weight,
    k_weight,
    q_moment,
    k_moment,
    q_weight_out,
    k_weight_out,
    q_moment_out,
    k_moment_out,
    *scratch,
):
    nx, nz, ny, nh, nc = sizes
    q_grad, k_grad, blocks, x_full, pairs, in_sem, send_sem, recv_sem = scratch[:8]
    bufs = scratch[8:]
    me = tuple(lax.axis_index(name) for name in AXES)
    rows = q_rows + k_rows

    def at(axis, shift):
        there = list(me)
        there[axis] = lax.rem(me[axis] + shift + sizes[axis], sizes[axis])
        return tuple(there)

    reads = [
        pltpu.make_async_copy(q_grad_hbm, q_grad, in_sem.at[0]),
        pltpu.make_async_copy(k_grad_hbm, k_grad, in_sem.at[1]),
    ]
    for read in reads:
        read.start()
    partners = []
    for axis in range(3):
        shifts = {1 % sizes[axis], sizes[axis] - 1}
        if axis == 0:
            shifts.add(nx // 2)
        partners += [at(axis, s) for s in sorted(shifts) if s]
    partners += [at(3, s) for s in range(1, nh)] + [at(4, s) for s in range(1, nc)]
    barrier = pltpu.get_barrier_semaphore()
    for there in partners:
        pl.semaphore_signal(
            barrier, inc=1, device_id=there, device_id_type=pl.DeviceIdType.MESH
        )

    place = me[3] * nc + me[4]
    lane = lax.broadcasted_iota(jnp.int32, (PEAK_ROWS, W), 1)
    token = lax.broadcasted_iota(jnp.int32, (tokens, picks), 0)
    peaks = jnp.full((PEAK_ROWS, W), LOWEST, jnp.float32)
    for h in range(local_heads):
        picked = []
        for pick, heads in ((q_pick, q_heads), (k_pick, k_heads)):
            chosen = (token == pick[h : h + 1, :]).astype(jnp.float32).astype(jnp.bfloat16)
            picked.append(contract_rows(chosen, heads[:, h * W : (h + 1) * W]))
        score = jnp.sum(picked[0] * picked[1], axis=1, keepdims=True)
        top = jnp.max(score, axis=0, keepdims=True) * SCORE_SCALE
        peaks = jnp.where(lane == place * local_heads + h, top, peaks)
    bufs[0][...] = peaks
    pl.semaphore_wait(barrier, len(partners))

    shaped, slot_of, sem_of, sems, pos = [], [], {}, 0, 0
    for i, stream in enumerate(streams):
        shaped.append(bufs[pos : pos + 6])
        pos += 6
        slots = {}
        for k in range(3):
            number = 0
            lengths = chains(sizes[stream["order"][k]], stream["parity"])
            for way, length in lengths.items():
                for t in range(length):
                    slots[k, way, t] = number
                    sem_of[i, k, way, t] = sems
                    number += 1
                    sems += 1
        slot_of.append(slots)

    for read in reads:
        read.wait()

    def terms(j, carry):
        x_low, z = j // nz, lax.rem(j, nz)
        cols = pl.ds(pl.multiple_of(j * (ny * W), ny * W), ny * W)
        out = (
            jnp.dot(q_lat[...], q_grad[:, cols], preferred_element_type=jnp.float32),
            jnp.dot(k_lat[...], k_grad[:, cols], preferred_element_type=jnp.float32),
        )
        for stream, buf in zip(streams, shaped):
            if stream["peak"]:
                continue
            for half in range(2):
                first = half * (q_rows, k_rows)[stream["kind"]] + stream["at"]
                for y in range(ny):
                    where = {0: half * (nx // 2) + x_low, 1: z, 2: y}
                    a, b, c = (where[axis] for axis in stream["order"])
                    buf[0][a, b, c] = out[stream["kind"]][
                        first : first + stream["rows"], y * W : (y + 1) * W
                    ]
        return carry

    lax.fori_loop(0, nx // 2 * nz, terms, 0)

    def join(stream, a, b):
        return jnp.maximum(a, b) if stream["peak"] else a + b

    def own_part(i, k, which):
        stream, buf = streams[i], shaped[i]
        source = (buf[0], buf[2], buf[4])[k]
        return source if stream["peak"] else source.at[which]

    def remote(i, k, way, t):
        stream, buf = streams[i], shaped[i]
        axis = stream["order"][k]
        landing = (buf[1], buf[3], buf[5])[k]
        length = chains(sizes[axis], stream["parity"])[way]
        if t == 0:
            which = lax.rem(me[axis] + way * length + sizes[axis], sizes[axis])
            source = own_part(i, k, which)
        else:
            source = landing.at[slot_of[i][k, way, t - 1]]
        sem = sem_of[i, k, way, t]
        return pltpu.make_async_remote_copy(
            src_ref=source,
            dst_ref=landing.at[slot_of[i][k, way, t]],
            send_sem=send_sem.at[sem],
            recv_sem=recv_sem.at[sem],
            device_id=at(axis, way),
            device_id_type=pl.DeviceIdType.MESH,
        )

    half = me[0] // (nx // 2)
    mine = blocks.at[half, me[3], me[4]]
    started = []
    for act in acts:
        if act[0] == "send":
            copy = remote(*act[1:])
            copy.start()
            started.append(copy)
        elif act[0] == "recv":
            _, i, k, way, t = act
            remote(i, k, way, t).wait_recv()
            stream = streams[i]
            axis = stream["order"][k]
            length = chains(sizes[axis], stream["parity"])[way]
            if t < length - 1:
                landed = (shaped[i][1], shaped[i][3], shaped[i][5])[k].at[slot_of[i][k, way, t]]
                which = lax.rem(me[axis] + way * (length - t - 1) + sizes[axis], sizes[axis])
                landed[...] = join(stream, landed[...], own_part(i, k, which)[...])
        else:
            _, i, k = act
            stream = streams[i]
            axis = stream["order"][k]
            total = own_part(i, k, me[axis])[...]
            landing = (shaped[i][1], shaped[i][3], shaped[i][5])[k]
            for way, length in chains(sizes[axis], stream["parity"]).items():
                if length > 0:
                    total = join(stream, total, landing[slot_of[i][k, way, length - 1]])
            if k < 2:
                (shaped[i][2], shaped[i][4])[k][...] = total
            elif stream["peak"]:
                mine[rows:, :] = total
            else:
                span = pl.ds(stream["at"], stream["rows"])
                moment, out = ((q_moment, q_moment_out), (k_moment, k_moment_out))[stream["kind"]]
                fresh = MOMENTUM * moment[span, :] + total
                out[span, :] = fresh
                mine[pl.ds(stream["kind"] * q_rows + stream["at"], stream["rows"]), :] = fresh

    gathered = sems
    sent = 0

    def hand_on(which, there):
        nonlocal sent
        h, y, c = which
        number = (h * nh + y) * nc + c
        copy = pltpu.make_async_remote_copy(
            src_ref=blocks.at[h, y, c],
            dst_ref=blocks.at[h, y, c],
            send_sem=send_sem.at[gathered + sent],
            recv_sem=recv_sem.at[gathered + number],
            device_id=there,
            device_id_type=pl.DeviceIdType.MESH,
        )
        copy.start()
        started.append(copy)
        sent += 1

    def arrived(which):
        h, y, c = which
        number = (h * nh + y) * nc + c
        pltpu.make_async_remote_copy(
            src_ref=blocks.at[h, y, c],
            dst_ref=blocks.at[h, y, c],
            send_sem=send_sem.at[gathered],
            recv_sem=recv_sem.at[gathered + number],
            device_id=me,
            device_id_type=pl.DeviceIdType.MESH,
        ).wait_recv()

    own = (half, me[3], me[4])
    far = (1 - half, me[3], me[4])
    hand_on(own, at(0, nx // 2))
    for s in range(1, nh):
        hand_on(own, at(3, s))
    for s in range(1, nc):
        hand_on(own, at(4, s))
    arrived(far)
    for s in range(1, nh):
        hand_on(far, at(3, s))
    for s in range(1, nc):
        hand_on(far, at(4, s))
    for h in (half, 1 - half):
        for s in range(1, nh):
            other = (h, lax.rem(me[3] - s + nh, nh), me[4])
            arrived(other)
            for s2 in range(1, nc):
                hand_on(other, at(4, s2))
    for s2 in range(1, nc):
        for h in (half, 1 - half):
            for s in range(nh):
                arrived((h, lax.rem(me[3] - s + nh, nh), lax.rem(me[4] - s2 + nc, nc)))
    for copy in started:
        copy.wait_send()

    head = lax.rem((me[0] * nz + me[1]) * ny + me[2], nx * nz * ny // 2)
    top = jnp.full((PEAK_ROWS, W), LOWEST, jnp.float32)
    for y in range(nh):
        for c in range(nc):
            top = jnp.maximum(top, blocks[half, y, c, rows:, :])
    top = jnp.where(lane == head, top, LOWEST)
    peak = jnp.max(jnp.max(top, axis=1, keepdims=True), axis=0, keepdims=True)
    shrink = jnp.sqrt(CLIP_LEVEL / jnp.maximum(peak, CLIP_LEVEL))

    count = 2 * nh * nc
    starts = (0, count * q_rows)
    heights = (count * q_rows, count * k_rows)
    for h in range(2):
        for y in range(nh):
            for c in range(nc):
                number = (h * nh + y) * nc + c
                block = blocks[h, y, c]
                for kind, part in ((0, block[:q_rows]), (1, block[q_rows:rows])):
                    height = (q_rows, k_rows)[kind]
                    span = pl.ds(starts[kind] + number * height, height)
                    x_full[span, :] = part
                    pairs[span, :] = split(part)

    def tile(kind):
        return pl.ds(starts[kind], heights[kind])

    eye = lax.broadcasted_iota(jnp.int32, (W, W), 0) == lax.broadcasted_iota(
        jnp.int32, (W, W), 1
    )
    mixers, scales = [], []
    for kind in range(2):
        gram = gramian(pairs[tile(kind), :])
        diagonal = jnp.where(eye, gram, 0.0)
        trace = jnp.sum(jnp.sum(diagonal, axis=1, keepdims=True), axis=0, keepdims=True)
        scale = 1.0 / jnp.sqrt(trace + 1.0)
        mixers.append(mixer_of(gram * (scale * scale)))
        scales.append(scale)
    for kind in range(2):
        fresh = scales[kind] * (
            COEFF_A * x_full[tile(kind), :] + mixed(pairs[tile(kind), :], mixers[kind])
        )
        x_full[tile(kind), :] = fresh
        pairs[tile(kind), :] = split(fresh)

    def iteration(_, carry):
        mixers = [mixer_of(gramian(pairs[tile(kind), :])) for kind in range(2)]
        for kind in range(2):
            fresh = COEFF_A * x_full[tile(kind), :] + mixed(pairs[tile(kind), :], mixers[kind])
            x_full[tile(kind), :] = fresh
            pairs[tile(kind), :] = split(fresh)
        return carry

    lax.fori_loop(0, ITERS - 2, iteration, 0)
    number = (half * nh + me[3]) * nc + me[4]
    keep = 1.0 - STEP_SIZE * DECAY
    for kind, (weight, out, rank) in enumerate(
        ((q_weight, q_weight_out, QR), (k_weight, k_weight_out, KR))
    ):
        height = (q_rows, k_rows)[kind]
        mixer = mixer_of(gramian(pairs[tile(kind), :]))
        span = pl.ds(pl.multiple_of(starts[kind] + number * height, 8), height)
        current = x_full[span, :]
        ortho = COEFF_A * current + mixed(split(current), mixer)
        out[...] = (weight[...] * keep - STEP_SIZE * 0.2 * math.sqrt(rank) * ortho) * shrink


def step(sizes, q_rows, k_rows, picks, tokens, local_heads):
    streams = make_streams(q_rows, k_rows)
    acts = plan(streams, sizes)
    rows = q_rows + k_rows
    width = sizes[0] * sizes[1] * sizes[2] // 2 * W
    count = 2 * sizes[3] * sizes[4]
    scratch = [
        pltpu.VMEM((tokens, width), jnp.bfloat16),
        pltpu.VMEM((tokens, width), jnp.bfloat16),
        pltpu.VMEM((2, sizes[3], sizes[4], rows + PEAK_ROWS, W), jnp.float32),
        pltpu.VMEM((count * rows, W), jnp.float32),
        pltpu.VMEM((count * rows, 2 * W), jnp.bfloat16),
        pltpu.SemaphoreType.DMA((2,)),
    ]
    messages = 0
    bufs = []
    for stream in streams:
        n = [sizes[axis] for axis in stream["order"]]
        messages += sum(n) - 3
        tile = (stream["rows"], W)
        lead = [(), (), ()] if stream["peak"] else [(n[1], n[2]), (n[2],), ()]
        for k in range(3):
            source = lead[k] if stream["peak"] else (n[k],) + lead[k]
            bufs.append(pltpu.VMEM(source + tile, jnp.float32))
            bufs.append(pltpu.VMEM((max(n[k] - 1, 1),) + lead[k] + tile, jnp.float32))
    scratch += [
        pltpu.SemaphoreType.DMA((messages + count,)),
        pltpu.SemaphoreType.DMA((messages + count,)),
    ]
    vmem = pl.BlockSpec(memory_space=pltpu.VMEM)
    hbm = pl.BlockSpec(memory_space=pl.ANY)
    return pl.pallas_call(
        functools.partial(
            body, sizes, q_rows, k_rows, picks, tokens, local_heads, streams, acts
        ),
        out_shape=[
            jax.ShapeDtypeStruct((q_rows, W), jnp.float32),
            jax.ShapeDtypeStruct((k_rows, W), jnp.float32),
            jax.ShapeDtypeStruct((q_rows, W), jnp.float32),
            jax.ShapeDtypeStruct((k_rows, W), jnp.float32),
        ],
        in_specs=[vmem, vmem, hbm, hbm] + [vmem] * 8,
        out_specs=[vmem] * 4,
        scratch_shapes=scratch + bufs,
        compiler_params=pltpu.CompilerParams(
            collective_id=0, has_side_effects=True, vmem_limit_bytes=60 * 1024 * 1024
        ),
        name="muon_clip",
    )


def local(
    sizes,
    q_latent,
    kv_latent,
    q_head_grad,
    k_head_grad,
    q_heads,
    k_heads,
    query_pick,
    key_pick,
    q_weight,
    k_weight,
    q_moment,
    k_moment,
):
    tokens, _, q_rows = q_latent.shape
    k_rows = kv_latent.shape[2]
    picks, local_heads = query_pick.shape[1:]
    out = step(sizes, q_rows, k_rows, picks, tokens, local_heads)(
        q_latent.transpose(1, 2, 0).reshape(2 * q_rows, tokens),
        kv_latent.transpose(1, 2, 0).reshape(2 * k_rows, tokens),
        q_head_grad,
        k_head_grad,
        q_heads,
        k_heads,
        query_pick[0].T,
        key_pick[0].T,
        q_weight[0],
        k_weight[0],
        q_moment[0],
        k_moment[0],
    )
    return tuple(array[None] for array in out)


def solution(mesh, sizes=SHAPE):
    axes = Mesh(mesh.devices.reshape(sizes), AXES)
    placed = (
        P(DP, None, MP),
        P(DP, None, MP),
        P(DP, None),
        P(DP, None),
        P(DP, MP),
        P(DP, MP),
        P(DP, None, MP),
        P(DP, None, MP),
        P(DP, MP, None),
        P(DP, MP, None),
        P(DP, MP, None),
        P(DP, MP, None),
    )
    return jax.shard_map(
        functools.partial(local, sizes),
        mesh=axes,
        in_specs=placed,
        out_specs=(P(DP, MP, None),) * 4,
        check_vma=False,
    )
```

time: 333 us -> 108 us (0.32)
  waiting for transfers between devices: 160 us -> 0 us
  Pallas kernels: 0 us -> 101 us
  blocking collectives: 74.4 us -> 0 us
  local copies, waits for them, and re-layouts: 41.4 us -> 6.79 us
  matrix products: 28.5 us -> 0 us
  between operations: 15.1 us -> 0.64 us
  other arithmetic: 7.99 us -> 0 us
  starting transfers between devices: 4.76 us -> 0 us
    reduce_scatter x3 -> x0, waiting for transfers between devices: 160 us -> none  [own_rows(): subtotal = lax.psum_scatter(subtotal, axis, scatter_dimension=0, tiled=True)]
    pallas_call x0 -> x1, Pallas kernels: none -> 101 us  [local(): step(sizes, q_rows, k_rows, picks, tokens, local_heads)]
    pmax x5 -> x0, blocking collectives: 57.2 us -> none  [over_axes(): value = lax.pmax(value, axis)]
    dot_general x32 -> x0, matrix products: 28.5 us -> none  [the longest x10 10.1 us: gramian(): return jnp.einsum('rc,rd->cd', matrix, matrix, precision=HIGHEST)]
    gather x12 -> x0, local copies, waits for them, and re-layouts: 21.2 us -> none  [the longest x1 7.9 us: local(): k_cols = jnp.take(k_grads, owners, axis=1)]
    all_gather x1 -> x0, blocking collectives: 17.2 us -> none  [gather_together(): lines, at, finished = (lax.all_gather(vector, axis), 0, [])]
    reshape x4 -> x0, local copies, waits for them, and re-layouts: 8.61 us -> none  [the longest x1 4.69 us: local(): k_grads = k_head_grad.reshape(tokens_here, head_count, width)]
    ppermute x1 -> x0, starting transfers between devices: 4.64 us -> none  [from_behind(): return lax.ppermute(value, axis, pairs)]
  transfers between devices with their start and end apart: 4 -> 0, of which waited for: 3 -> 0; matrix products, arithmetic and copies ran while one was open for 2% -> 0% of each run, Pallas kernels for 0% -> 0%
where the time goes in v1:
time: 108 us
  Pallas kernels  101 us (94%)
  local copies, waits for them, and re-layouts  6.79 us (6%)
    pallas_call x1, Pallas kernels, local(): step(sizes, q_rows, k_rows, picks, tokens, local_heads)  101 us
    unnamed x4, local copies, waits for them, and re-layouts  5.49 us

profile of v1, /device:TPU:1, one launch (start us, length us, event | category | flops | bytes accessed | tf_op | source)
XLA Modules:
  0.0 108.1 jit_solution(16936262808082025708)
XLA Ops:
  0.6 1.3 %copy_bitcast_fusion = (s32[6,16]{1,0:T(8,128)}, s32[6,16]{1,0:T(8,128)}) fusion(s32[1,16,6]{1,0,2:T(1,128)} %param.19, s32[1,16,6]{1,0,2:T(1,128)} %param.18), kind=kLoop, calls=%fused_computation | loop fusion | bytes 1536 | tf_op jit(solution)/shard_map/transpose | solution.py:530
  1.9 100.6 %muon_clip.1 = (f32[96,128]{1,0:T(8,128)}, f32[32,128]{1,0:T(8,128)}, f32[96,128]{1,0:T(8,128)}, f32[32,128]{1,0:T(8,128)}) custom-call(bf16[192,256]{1,0:T(8,128)(2,1)} %bitcast.22, bf16[64,256]{1,0:T(8,128)(2,1)} %bitcast.27, bf16[256,6144]{1,0:T(8,128)(2,1)} %q_grad_hbm.1, bf16[256,6144]{1,0:T(8,128)(2,1)} %k_grad_hbm.1, bf16[256,768]{1,0:T(8,128)(2,1)} %q_heads.1, ...), custom_call_target="tpu_custom_call" | custom-call | tf_op jit(solution)/shard_map/muon_clip/pallas_call | solution.py:522
  102.6 1.4 %copy.24 = f32[1,96,128]{2,1,0:T(8,128)} copy(f32[1,96,128]{2,1,0:T(8,128)} %bitcast.26) | data formatting | bytes 98304
  104.0 1.3 %copy.25 = f32[1,32,128]{2,1,0:T(8,128)} copy(f32[1,32,128]{2,1,0:T(8,128)} %bitcast.31) | data formatting | bytes 32768
  105.3 1.4 %copy.26 = f32[1,96,128]{2,1,0:T(8,128)} copy(f32[1,96,128]{2,1,0:T(8,128)} %bitcast.25) | data formatting | bytes 98304
  106.7 1.3 %copy.27 = f32[1,32,128]{2,1,0:T(8,128)} copy(f32[1,32,128]{2,1,0:T(8,128)} %bitcast.30) | data formatting | bytes 32768

commit v2 on v1

--- a/solution.py
+++ b/solution.py
@@ -44,7 +44,7 @@
     return size
 
 
-def plan(streams, sizes, rate=46.6e3, latency=2.4, backlog=8.0, turn=0.15):
+def plan(streams, sizes, rate=46.6e3, latency=2.4, backlog=8.0, turn=0.15, rest=3.5):
     free, pool, acts, events, left = {}, [], [], [], {}
     count = 0
 
@@ -74,9 +74,16 @@
                 kept.append(item)
         pool[:] = kept
 
+    early = [i for i, stream in enumerate(streams) if stream["order"][0] == 1]
     now = 0.0
+    for i in early:
+        start_stage(i, 0)
+    fill(now)
+    acts.append(("rest",))
+    now = rest
     for i in range(len(streams)):
-        start_stage(i, 0)
+        if i not in early:
+            start_stage(i, 0)
     fill(now)
     while events:
         at, _, (i, k, way, t) = heapq.heappop(events)
@@ -187,12 +194,29 @@
         there[axis] = lax.rem(me[axis] + shift + sizes[axis], sizes[axis])
         return tuple(there)
 
-    reads = [
-        pltpu.make_async_copy(q_grad_hbm, q_grad, in_sem.at[0]),
-        pltpu.make_async_copy(k_grad_hbm, k_grad, in_sem.at[1]),
-    ]
-    for read in reads:
-        read.start()
+    def nth_z(n):
+        size = nz // 2 - (n + 1) // 2
+        return lax.rem(me[1] + (size if n % 2 else -size) + nz, nz)
+
+    def loop_z(n):
+        size = nz // 2 - (n + 1) // 2
+        return lax.rem(me[1] + jnp.where(lax.rem(n, 2) == 1, size, -size) + nz, nz)
+
+    def reads(n, z):
+        copies = []
+        for x_low in range(nx // 2):
+            cols = pl.ds(pl.multiple_of((x_low * nz + z) * (ny * W), ny * W), ny * W)
+            for kind, (source, target) in enumerate(((q_grad_hbm, q_grad), (k_grad_hbm, k_grad))):
+                copies.append(
+                    pltpu.make_async_copy(
+                        source.at[:, cols], target.at[:, cols], in_sem.at[n, x_low, kind]
+                    )
+                )
+        return copies
+
+    for n in range(nz):
+        for copy in reads(n, nth_z(n)):
+            copy.start()
     partners = []
     for axis in range(3):
         shifts = {1 % sizes[axis], sizes[axis] - 1}
@@ -213,13 +237,12 @@
     for h in range(local_heads):
         picked = []
         for pick, heads in ((q_pick, q_heads), (k_pick, k_heads)):
-            chosen = (token == pick[h : h + 1, :]).astype(jnp.float32).astype(jnp.bfloat16)
+            chosen = (token == pick[h]).astype(jnp.float32).astype(jnp.bfloat16)
             picked.append(contract_rows(chosen, heads[:, h * W : (h + 1) * W]))
         score = jnp.sum(picked[0] * picked[1], axis=1, keepdims=True)
         top = jnp.max(score, axis=0, keepdims=True) * SCORE_SCALE
         peaks = jnp.where(lane == place * local_heads + h, top, peaks)
     bufs[0][...] = peaks
-    pl.semaphore_wait(barrier, len(partners))
 
     shaped, slot_of, sem_of, sems, pos = [], [], {}, 0, 0
     for i, stream in enumerate(streams):
@@ -237,30 +260,42 @@
                     sems += 1
         slot_of.append(slots)
 
-    for read in reads:
-        read.wait()
-
-    def terms(j, carry):
-        x_low, z = j // nz, lax.rem(j, nz)
-        cols = pl.ds(pl.multiple_of(j * (ny * W), ny * W), ny * W)
-        out = (
-            jnp.dot(q_lat[...], q_grad[:, cols], preferred_element_type=jnp.float32),
-            jnp.dot(k_lat[...], k_grad[:, cols], preferred_element_type=jnp.float32),
-        )
-        for stream, buf in zip(streams, shaped):
-            if stream["peak"]:
-                continue
-            for half in range(2):
-                first = half * (q_rows, k_rows)[stream["kind"]] + stream["at"]
-                for y in range(ny):
-                    where = {0: half * (nx // 2) + x_low, 1: z, 2: y}
-                    a, b, c = (where[axis] for axis in stream["order"])
-                    buf[0][a, b, c] = out[stream["kind"]][
-                        first : first + stream["rows"], y * W : (y + 1) * W
-                    ]
-        return carry
-
-    lax.fori_loop(0, nx // 2 * nz, terms, 0)
+    def terms(n, z):
+        for copy in reads(n, z):
+            copy.wait()
+        for x_low in range(nx // 2):
+            cols = pl.ds(pl.multiple_of((x_low * nz + z) * (ny * W), ny * W), ny * W)
+            out = (
+                jnp.dot(q_lat[...], q_grad[:, cols], preferred_element_type=jnp.float32),
+                jnp.dot(k_lat[...], k_grad[:, cols], preferred_element_type=jnp.float32),
+            )
+            for stream, buf in zip(streams, shaped):
+                if stream["peak"]:
+                    continue
+                for half in range(2):
+                    first = half * (q_rows, k_rows)[stream["kind"]] + stream["at"]
+                    for y in range(ny):
+                        where = {0: half * (nx // 2) + x_low, 1: z, 2: y}
+                        a, b, c = (where[axis] for axis in stream["order"])
+                        buf[0][a, b, c] = out[stream["kind"]][
+                            first : first + stream["rows"], y * W : (y + 1) * W
+                        ]
+
+    lead = min(3, nz)
+    for n in range(lead):
+        terms(n, nth_z(n))
+    pl.semaphore_wait(barrier, len(partners))
+
+    def rest_of_terms():
+        group = 3 if (nz - lead) % 3 == 0 else 1
+
+        def some(m, carry):
+            for g in range(group):
+                n = lead + m * group + g
+                terms(n, loop_z(n))
+            return carry
+
+        lax.fori_loop(0, (nz - lead) // group, some, 0)
 
     def join(stream, a, b):
         return jnp.maximum(a, b) if stream["peak"] else a + b
@@ -294,7 +329,9 @@
     mine = blocks.at[half, me[3], me[4]]
     started = []
     for act in acts:
-        if act[0] == "send":
+        if act[0] == "rest":
+            rest_of_terms()
+        elif act[0] == "send":
             copy = remote(*act[1:])
             copy.start()
             started.append(copy)
@@ -381,8 +418,6 @@
         for h in (half, 1 - half):
             for s in range(nh):
                 arrived((h, lax.rem(me[3] - s + nh, nh), lax.rem(me[4] - s2 + nc, nc)))
-    for copy in started:
-        copy.wait_send()
 
     head = lax.rem((me[0] * nz + me[1]) * ny + me[2], nx * nz * ny // 2)
     top = jnp.full((PEAK_ROWS, W), LOWEST, jnp.float32)
@@ -448,6 +483,8 @@
         current = x_full[span, :]
         ortho = COEFF_A * current + mixed(split(current), mixer)
         out[...] = (weight[...] * keep - STEP_SIZE * 0.2 * math.sqrt(rank) * ortho) * shrink
+    for copy in started:
+        copy.wait_send()
 
 
 def step(sizes, q_rows, k_rows, picks, tokens, local_heads):
@@ -462,7 +499,7 @@
         pltpu.VMEM((2, sizes[3], sizes[4], rows + PEAK_ROWS, W), jnp.float32),
         pltpu.VMEM((count * rows, W), jnp.float32),
         pltpu.VMEM((count * rows, 2 * W), jnp.bfloat16),
-        pltpu.SemaphoreType.DMA((2,)),
+        pltpu.SemaphoreType.DMA((sizes[1], sizes[0] // 2, 2)),
     ]
     messages = 0
     bufs = []
@@ -480,16 +517,16 @@
         pltpu.SemaphoreType.DMA((messages + count,)),
     ]
     vmem = pl.BlockSpec(memory_space=pltpu.VMEM)
-    hbm = pl.BlockSpec(memory_space=pl.ANY)
+    hbm = pl.BlockSpec(memory_space=pltpu.HBM)
     return pl.pallas_call(
         functools.partial(
             body, sizes, q_rows, k_rows, picks, tokens, local_heads, streams, acts
         ),
         out_shape=[
-            jax.ShapeDtypeStruct((q_rows, W), jnp.float32),
-            jax.ShapeDtypeStruct((k_rows, W), jnp.float32),
-            jax.ShapeDtypeStruct((q_rows, W), jnp.float32),
-            jax.ShapeDtypeStruct((k_rows, W), jnp.float32),
+            pltpu.VMEM((q_rows, W), jnp.float32),
+            pltpu.VMEM((k_rows, W), jnp.float32),
+            pltpu.VMEM((q_rows, W), jnp.float32),
+            pltpu.VMEM((k_rows, W), jnp.float32),
         ],
         in_specs=[vmem, vmem, hbm, hbm] + [vmem] * 8,
         out_specs=[vmem] * 4,
@@ -499,6 +536,23 @@
         ),
         name="muon_clip",
     )
+
+
+def hand_out(*refs):
+    for source, target in zip(refs[:4], refs[4:]):
+        target[...] = source[...]
+
+
+def handed_out(arrays):
+    vmem = pl.BlockSpec(memory_space=pltpu.VMEM)
+    return pl.pallas_call(
+        hand_out,
+        out_shape=[jax.ShapeDtypeStruct(a.shape, a.dtype) for a in arrays],
+        in_specs=[vmem] * 4,
+        out_specs=[vmem] * 4,
+        compiler_params=pltpu.CompilerParams(vmem_limit_bytes=2 * 1024 * 1024),
+        name="hand_out",
+    )(*arrays)
 
 
 def local(
@@ -526,14 +580,14 @@
         k_head_grad,
         q_heads,
         k_heads,
-        query_pick[0].T,
-        key_pick[0].T,
+        query_pick.transpose(2, 0, 1),
+        key_pick.transpose(2, 0, 1),
         q_weight[0],
         k_weight[0],
         q_moment[0],
         k_moment[0],
     )
-    return tuple(array[None] for array in out)
+    return tuple(array[None] for array in handed_out(out))
 
 
 def solution(mesh, sizes=SHAPE):

time: 108 us -> 99.1 us (0.918)
  local copies, waits for them, and re-layouts: 6.79 us -> 0 us
  Pallas kernels: 101 us -> 98.3 us
    unnamed x4 -> x0, local copies, waits for them, and re-layouts: 5.49 us -> none
    pallas_call x1, Pallas kernels: 101 us -> 97.6 us  [local(): step(sizes, q_rows, k_rows, picks, tokens, local_heads)]
    transpose x1 -> x0, local copies, waits for them, and re-layouts: 1.3 us -> none  [local(): key_pick[0]]
where the time goes in v2:
time: 99.1 us; the launch traced here: 98.9 us
  Pallas kernels  98.3 us (99%)
    pallas_call x1, Pallas kernels, local(): step(sizes, q_rows, k_rows, picks, tokens, local_heads)  97.6 us

profile of v2, /device:TPU:1, one launch (start us, length us, event | category | flops | bytes accessed | tf_op | source)
XLA Modules:
  0.0 98.9 jit_solution(12243956576185664457)
XLA Ops:
  0.6 97.6 %muon_clip.1 = (f32[96,128]{1,0:T(8,128)S(1)}, f32[32,128]{1,0:T(8,128)S(1)}, f32[96,128]{1,0:T(8,128)S(1)}, f32[32,128]{1,0:T(8,128)S(1)}) custom-call(bf16[192,256]{1,0:T(8,128)(2,1)} %bitcast.16, bf16[64,256]{1,0:T(8,128)(2,1)} %bitcast.19, bf16[256,6144]{1,0:T(8,128)(2,1)} %q_grad_hbm.1, bf16[256,6144]{1,0:T(8,128)(2,1)} %k_grad_hbm.1, ...), custom_call_target="tpu_custom_call" | custom-call | tf_op jit(solution)/shard_map/muon_clip/pallas_call | solution.py:576
  98.3 0.7 hand_out.1

commit v3 on v2

--- a/solution.py
+++ b/solution.py
@@ -31,9 +31,27 @@
 PEAK_ROWS = 8
 
 
-def chains(n, parity):
+TREES = {
+    2: ((2, 0), (1, 0)),
+    3: ((1, 0), (3, 2), (2, 0)),
+    5: ((1, 0), (3, 2), (5, 4), (4, 2), (2, 0)),
+    6: ((1, 0), (3, 2), (5, 4), (6, 4), (4, 2), (2, 0)),
+}
+
+
+def routes(n, parity, short):
     far, near = n // 2, n - 1 - n // 2
-    return {-1: far, 1: near} if parity == 0 else {-1: near, 1: far}
+    lengths = {-1: far, 1: near} if parity == 0 else {-1: near, 1: far}
+    found = {}
+    for way, length in lengths.items():
+        if length:
+            chain = tuple((f, f - 1) for f in range(length, 0, -1))
+            found[way] = TREES.get(length, chain) if short else chain
+    return found
+
+
+def stage_routes(stream, stage, sizes):
+    return routes(sizes[stream["order"][stage]], stream["parity"], stream["short"][stage])
 
 
 def message_bytes(stream, stage, sizes):
@@ -44,41 +62,63 @@
     return size
 
 
-def plan(streams, sizes, rate=46.6e3, latency=2.4, backlog=8.0, turn=0.15, rest=3.5):
-    free, pool, acts, events, left = {}, [], [], [], {}
+def plan(streams, sizes, rate=47.5e3, latency=2.5, hop=0.75, backlog=5.0, turn=0.12, rest=3.5):
+    free, pool, acts, events, left, missing = {}, [], [], [], {}, {}
     count = 0
+    ways = [[stage_routes(stream, k, sizes) for k in range(3)] for stream in streams]
+
+    def sent_to(i, k, way, f):
+        return dict(ways[i][k][way])[f]
+
+    def lasts(i, k, way, f):
+        time = 0.0
+        while f > 0:
+            g = sent_to(i, k, way, f)
+            time += latency + turn + (f - g - 1) * hop
+            time += (f - g) * message_bytes(streams[i], k, sizes) / rate
+            f = g
+        return time
+
+    def add(i, k, way, f):
+        time = lasts(i, k, way, f)
+        for later in range(k + 1, 3):
+            time += max(
+                lasts(i, later, w, start) for w, pairs in ways[i][later].items() for start, _ in pairs
+            )
+        pool.append((i - time + streams[i]["offset"], (i, k, way, f)))
 
     def start_stage(i, k):
-        stream = streams[i]
-        lengths = chains(sizes[stream["order"][k]], stream["parity"])
-        left[i, k] = sum(length > 0 for length in lengths.values())
-        for way, length in lengths.items():
-            if length > 0:
-                pool.append(((-k if k else 1, -length if k == 0 else 0, i), (i, k, way, 0)))
+        left[i, k] = 0
+        for way, pairs in ways[i][k].items():
+            for f, _ in pairs:
+                missing[i, k, way, f] = sum(g == f for _, g in pairs)
+                if missing[i, k, way, f] == 0:
+                    add(i, k, way, f)
+            left[i, k] += sum(g == 0 for _, g in pairs)
 
     def fill(now):
         nonlocal count
         pool.sort()
         kept = []
         for item in pool:
-            i, k, way, _ = item[1]
+            i, k, way, f = item[1]
             axis = streams[i]["order"][k]
             link = (axis, way if sizes[axis] > 2 else 0)
             if free.get(link, 0.0) - now < backlog:
+                hops = f - sent_to(i, k, way, f)
                 begin = max(free.get(link, 0.0), now)
-                free[link] = begin + message_bytes(streams[i], k, sizes) / rate
+                free[link] = begin + hops * message_bytes(streams[i], k, sizes) / rate
                 count += 1
-                heapq.heappush(events, (free[link] + latency, count, item[1]))
+                heapq.heappush(events, (free[link] + latency + (hops - 1) * hop, count, item[1]))
                 acts.append(("send",) + item[1])
             else:
                 kept.append(item)
         pool[:] = kept
 
     early = [i for i, stream in enumerate(streams) if stream["order"][0] == 1]
-    now = 0.0
     for i in early:
         start_stage(i, 0)
-    fill(now)
+    fill(0.0)
     acts.append(("rest",))
     now = rest
     for i in range(len(streams)):
@@ -86,13 +126,15 @@
             start_stage(i, 0)
     fill(now)
     while events:
-        at, _, (i, k, way, t) = heapq.heappop(events)
+        at, _, (i, k, way, f) = heapq.heappop(events)
         now = max(now, at) + turn
-        stream = streams[i]
-        length = chains(sizes[stream["order"][k]], stream["parity"])[way]
-        acts.append(("recv", i, k, way, t))
-        if t < length - 1:
-            pool.append(((-k if k else 0, -(length - t), i), (i, k, way, t + 1)))
+        g = sent_to(i, k, way, f)
+        acts.append(("recv", i, k, way, f))
+        if g > 0:
+            missing[i, k, way, g] -= 1
+            if missing[i, k, way, g] == 0:
+                acts.append(("join", i, k, way, g))
+                add(i, k, way, g)
         else:
             left[i, k] -= 1
             if left[i, k] == 0:
@@ -103,28 +145,43 @@
     return acts
 
 
+X, Z, Y = 0, 1, 2
+PIECES = (
+    (1, (1, 2, 1), (Y, X, Z), (False, False, True), -2.53),
+    (0, (2, 3), (X, Y, Z), (False, True, True), 1.68),
+    (0, (1, 3, 3), (Z, Y, X), (False, True, True), 2.01),
+)
+
+
 def make_streams(q_rows, k_rows):
-    piece = q_rows // 6
-    streams = [dict(peak=True, rows=PEAK_ROWS, order=(0, 2, 1), parity=0)]
-    for n in range(4):
-        streams.append(
-            dict(peak=False, kind=0, at=n * piece, rows=piece, order=(0, 2, 1), parity=n % 2)
+    streams = [
+        dict(
+            peak=True,
+            rows=PEAK_ROWS,
+            order=(Z, X, Y),
+            parity=0,
+            short=(True, True, True),
+            offset=0.0,
         )
-    for n in range(4, 6):
-        streams.append(
-            dict(peak=False, kind=0, at=n * piece, rows=piece, order=(1, 0, 2), parity=n % 2)
-        )
-    for n in range(2):
-        streams.append(
-            dict(
-                peak=False,
-                kind=1,
-                at=n * (k_rows // 2),
-                rows=k_rows // 2,
-                order=(1, 0, 2),
-                parity=n % 2,
+    ]
+    used = [0, 0]
+    for kind, heights, order, short, offset in PIECES:
+        for n, height in enumerate(heights):
+            rows = height * (q_rows // 12, k_rows // 4)[kind]
+            streams.append(
+                dict(
+                    peak=False,
+                    kind=kind,
+                    at=used[kind],
+                    rows=rows,
+                    order=order,
+                    parity=n % 2,
+                    short=short,
+                    offset=offset,
+                )
             )
-        )
+            used[kind] += rows
+    assert used == [q_rows, k_rows]
     return streams
 
 
@@ -219,9 +276,11 @@
             copy.start()
     partners = []
     for axis in range(3):
-        shifts = {1 % sizes[axis], sizes[axis] - 1}
-        if axis == 0:
-            shifts.add(nx // 2)
+        shifts = {nx // 2} if axis == 0 else set()
+        for stream in streams:
+            for way, moves in stage_routes(stream, stream["order"].index(axis), sizes).items():
+                for f, g in moves:
+                    shifts |= {(f - g) % sizes[axis], (g - f) % sizes[axis]}
         partners += [at(axis, s) for s in sorted(shifts) if s]
     partners += [at(3, s) for s in range(1, nh)] + [at(4, s) for s in range(1, nc)]
     barrier = pltpu.get_barrier_semaphore()
@@ -251,11 +310,10 @@
         slots = {}
         for k in range(3):
             number = 0
-            lengths = chains(sizes[stream["order"][k]], stream["parity"])
-            for way, length in lengths.items():
-                for t in range(length):
-                    slots[k, way, t] = number
-                    sem_of[i, k, way, t] = sems
+            for way, moves in stage_routes(stream, k, sizes).items():
+                for f, _ in moves:
+                    slots[k, way, f] = number
+                    sem_of[i, k, way, f] = sems
                     number += 1
                     sems += 1
         slot_of.append(slots)
@@ -305,23 +363,28 @@
         source = (buf[0], buf[2], buf[4])[k]
         return source if stream["peak"] else source.at[which]
 
-    def remote(i, k, way, t):
-        stream, buf = streams[i], shaped[i]
-        axis = stream["order"][k]
-        landing = (buf[1], buf[3], buf[5])[k]
-        length = chains(sizes[axis], stream["parity"])[way]
-        if t == 0:
-            which = lax.rem(me[axis] + way * length + sizes[axis], sizes[axis])
-            source = own_part(i, k, which)
-        else:
-            source = landing.at[slot_of[i][k, way, t - 1]]
-        sem = sem_of[i, k, way, t]
+    def landing(i, k):
+        return (shaped[i][1], shaped[i][3], shaped[i][5])[k]
+
+    def incoming(i, k, way, g):
+        moves = stage_routes(streams[i], k, sizes).get(way, ())
+        return [landing(i, k).at[slot_of[i][k, way, f]] for f, to in moves if to == g]
+
+    def owner(i, k, way, f):
+        axis = streams[i]["order"][k]
+        return lax.rem(me[axis] + way * f + sizes[axis], sizes[axis])
+
+    def remote(i, k, way, f):
+        g = dict(stage_routes(streams[i], k, sizes)[way])[f]
+        joined = incoming(i, k, way, f)
+        source = joined[0] if joined else own_part(i, k, owner(i, k, way, f))
+        sem = sem_of[i, k, way, f]
         return pltpu.make_async_remote_copy(
             src_ref=source,
-            dst_ref=landing.at[slot_of[i][k, way, t]],
+            dst_ref=landing(i, k).at[slot_of[i][k, way, f]],
             send_sem=send_sem.at[sem],
             recv_sem=recv_sem.at[sem],
-            device_id=at(axis, way),
+            device_id=at(streams[i]["order"][k], way * (f - g)),
             device_id_type=pl.DeviceIdType.MESH,
         )
 
@@ -336,24 +399,21 @@
             copy.start()
             started.append(copy)
         elif act[0] == "recv":
-            _, i, k, way, t = act
-            remote(i, k, way, t).wait_recv()
-            stream = streams[i]
-            axis = stream["order"][k]
-            length = chains(sizes[axis], stream["parity"])[way]
-            if t < length - 1:
-                landed = (shaped[i][1], shaped[i][3], shaped[i][5])[k].at[slot_of[i][k, way, t]]
-                which = lax.rem(me[axis] + way * (length - t - 1) + sizes[axis], sizes[axis])
-                landed[...] = join(stream, landed[...], own_part(i, k, which)[...])
+            remote(*act[1:]).wait_recv()
+        elif act[0] == "join":
+            _, i, k, way, g = act
+            landed = incoming(i, k, way, g)
+            total = own_part(i, k, owner(i, k, way, g))[...]
+            for part in landed:
+                total = join(streams[i], total, part[...])
+            landed[0][...] = total
         else:
             _, i, k = act
             stream = streams[i]
-            axis = stream["order"][k]
-            total = own_part(i, k, me[axis])[...]
-            landing = (shaped[i][1], shaped[i][3], shaped[i][5])[k]
-            for way, length in chains(sizes[axis], stream["parity"]).items():
-                if length > 0:
-                    total = join(stream, total, landing[slot_of[i][k, way, length - 1]])
+            total = own_part(i, k, me[stream["order"][k]])[...]
+            for way in (-1, 1):
+                for part in incoming(i, k, way, 0):
+                    total = join(stream, total, part[...])
             if k < 2:
                 (shaped[i][2], shaped[i][4])[k][...] = total
             elif stream["peak"]:

time: 99.1 us -> 87.2 us (0.88)
  Pallas kernels: 98.3 us -> 86.4 us
    pallas_call x1, Pallas kernels: 97.6 us -> 85.8 us  [local(): step(sizes, q_rows, k_rows, picks, tokens, local_heads)]
where the time goes in v3:
time: 87.2 us; the launch traced here: 87.1 us
  Pallas kernels  86.4 us (99%)
    pallas_call x1, Pallas kernels, local(): step(sizes, q_rows, k_rows, picks, tokens, local_heads)  85.8 us

profile of v3, /device:TPU:1, one launch (start us, length us, event | category | flops | bytes accessed | tf_op | source)
XLA Modules:
  0.0 87.1 jit_solution(18295933239522764761)
XLA Ops:
  0.6 85.8 %muon_clip.1 = (f32[96,128]{1,0:T(8,128)S(1)}, f32[32,128]{1,0:T(8,128)S(1)}, f32[96,128]{1,0:T(8,128)S(1)}, f32[32,128]{1,0:T(8,128)S(1)}) custom-call(bf16[192,256]{1,0:T(8,128)(2,1)} %bitcast.16, bf16[64,256]{1,0:T(8,128)(2,1)} %bitcast.19, bf16[256,6144]{1,0:T(8,128)(2,1)} %q_grad_hbm.1, bf16[256,6144]{1,0:T(8,128)(2,1)} %k_grad_hbm.1, ...), custom_call_target="tpu_custom_call" | custom-call | tf_op jit(solution)/shard_map/muon_clip/pallas_call | solution.py:636
  86.4 0.7 hand_out.1

commit v4 on v3

--- a/solution.py
+++ b/solution.py
@@ -31,27 +31,33 @@
 PEAK_ROWS = 8
 
 
-TREES = {
+SHORT = {
+    1: ((1, 0),),
     2: ((2, 0), (1, 0)),
     3: ((1, 0), (3, 2), (2, 0)),
     5: ((1, 0), (3, 2), (5, 4), (4, 2), (2, 0)),
     6: ((1, 0), (3, 2), (5, 4), (6, 4), (4, 2), (2, 0)),
 }
-
-
-def routes(n, parity, short):
+FLAT = {
+    **SHORT,
+    5: ((3, 2), (1, 2), (5, 4), (4, 0), (2, 0)),
+    6: ((3, 2), (1, 2), (6, 5), (4, 5), (5, 0), (2, 0)),
+}
+
+
+def routes(n, parity, form):
     far, near = n // 2, n - 1 - n // 2
     lengths = {-1: far, 1: near} if parity == 0 else {-1: near, 1: far}
     found = {}
     for way, length in lengths.items():
         if length:
             chain = tuple((f, f - 1) for f in range(length, 0, -1))
-            found[way] = TREES.get(length, chain) if short else chain
+            found[way] = ({}, SHORT, FLAT)[form].get(length, chain)
     return found
 
 
 def stage_routes(stream, stage, sizes):
-    return routes(sizes[stream["order"][stage]], stream["parity"], stream["short"][stage])
+    return routes(sizes[stream["order"][stage]], stream["parity"], stream["forms"][stage])
 
 
 def message_bytes(stream, stage, sizes):
@@ -62,10 +68,16 @@
     return size
 
 
-def plan(streams, sizes, rate=47.5e3, latency=2.5, hop=0.75, backlog=5.0, turn=0.12, rest=3.5):
+def plan(
+    streams, groups, sizes, rate=47.5e3, latency=2.5, hop=0.75, backlog=5.0, turn=0.12, rest=3.5
+):
     free, pool, acts, events, left, missing = {}, [], [], [], {}, {}
     count = 0
     ways = [[stage_routes(stream, k, sizes) for k in range(3)] for stream in streams]
+    unfinished = [len(members) for members in groups]
+    group_of = {i: g for g, members in enumerate(groups) for i in members}
+    group_bytes = [sum(streams[i]["rows"] for i in members) * W * 4 for members in groups]
+    shifts = sorted(range(1, sizes[3]), key=lambda s: abs(2 * s - sizes[3]))
 
     def sent_to(i, k, way, f):
         return dict(ways[i][k][way])[f]
@@ -80,12 +92,12 @@
         return time
 
     def add(i, k, way, f):
-        time = lasts(i, k, way, f)
+        time = lasts(i, k, way, f) + 9.0
         for later in range(k + 1, 3):
             time += max(
                 lasts(i, later, w, start) for w, pairs in ways[i][later].items() for start, _ in pairs
             )
-        pool.append((i - time + streams[i]["offset"], (i, k, way, f)))
+        pool.append((i - time + streams[i]["offset"], ("sum", i, k, way, f)))
 
     def start_stage(i, k):
         left[i, k] = 0
@@ -96,26 +108,44 @@
                     add(i, k, way, f)
             left[i, k] += sum(g == 0 for _, g in pairs)
 
+    def load(message):
+        if message[0] == "sum":
+            _, i, k, way, f = message
+            axis = streams[i]["order"][k]
+            hops = f - sent_to(i, k, way, f)
+            size = hops * message_bytes(streams[i], k, sizes)
+            both = (("y", 1), ("y", -1))
+            return [(link, size) for link in (both if axis == 2 else ((axis, way),))], hops
+        size = group_bytes[message[1]]
+        if message[0] == "across":
+            return [((0, 1), size), ((0, -1), size)], 2
+        s, half = 2 * message[2], sizes[3]
+        taken = [((0, 1), size), ((0, -1), size)] if message[0] == "cross" else []
+        hops = 2 if message[0] == "cross" else 0
+        if s == half:
+            return taken + [(("y", 1), 2 * size), (("y", -1), 2 * size)], hops + 4
+        return taken + [(("y", 1 if s < half else -1), 2 * size)], hops + 2
+
     def fill(now):
         nonlocal count
         pool.sort()
         kept = []
         for item in pool:
-            i, k, way, f = item[1]
-            axis = streams[i]["order"][k]
-            link = (axis, way if sizes[axis] > 2 else 0)
-            if free.get(link, 0.0) - now < backlog:
-                hops = f - sent_to(i, k, way, f)
-                begin = max(free.get(link, 0.0), now)
-                free[link] = begin + hops * message_bytes(streams[i], k, sizes) / rate
+            taken, hops = load(item[1])
+            if max(free.get(link, 0.0) for link, _ in taken) - now < backlog:
+                end = 0.0
+                for link, size in taken:
+                    free[link] = max(free.get(link, 0.0), now) + size / rate
+                    end = max(end, free[link])
                 count += 1
-                heapq.heappush(events, (free[link] + latency + (hops - 1) * hop, count, item[1]))
-                acts.append(("send",) + item[1])
+                heapq.heappush(events, (end + latency + (hops - 1) * hop, count, item[1]))
+                acts.append(("send", item[1]))
             else:
                 kept.append(item)
         pool[:] = kept
 
     early = [i for i, stream in enumerate(streams) if stream["order"][0] == 1]
+    assert 0 not in early
     for i in early:
         start_stage(i, 0)
     fill(0.0)
@@ -126,31 +156,48 @@
             start_stage(i, 0)
     fill(now)
     while events:
-        at, _, (i, k, way, f) = heapq.heappop(events)
+        at, _, message = heapq.heappop(events)
         now = max(now, at) + turn
-        g = sent_to(i, k, way, f)
-        acts.append(("recv", i, k, way, f))
-        if g > 0:
-            missing[i, k, way, g] -= 1
-            if missing[i, k, way, g] == 0:
-                acts.append(("join", i, k, way, g))
-                add(i, k, way, g)
-        else:
-            left[i, k] -= 1
-            if left[i, k] == 0:
-                acts.append(("close", i, k))
-                if k < 2:
-                    start_stage(i, k + 1)
+        acts.append(("recv", message))
+        if message[0] == "sum":
+            _, i, k, way, f = message
+            g = sent_to(i, k, way, f)
+            if g > 0:
+                missing[i, k, way, g] -= 1
+                if missing[i, k, way, g] == 0:
+                    acts.append(("join", i, k, way, g))
+                    add(i, k, way, g)
+            else:
+                left[i, k] -= 1
+                if left[i, k] == 0:
+                    acts.append(("close", i, k))
+                    if k < 2:
+                        start_stage(i, k + 1)
+                    else:
+                        ready = group_of[i]
+                        unfinished[ready] -= 1
+                        if unfinished[ready] == 0:
+                            acts.append(("ready", ready))
+                            pool.append((-31.0, ("across", ready)))
+                            for n, s in enumerate(shifts):
+                                pool.append((-21.0 + min(n, 1), ("own", ready, s)))
+                                if ready not in RELAYED:
+                                    pool.append((-16.0 + min(n, 1), ("cross", ready, s)))
+        elif message[0] == "across" and message[1] in RELAYED:
+            for n, s in enumerate(shifts):
+                pool.append((-11.0 + min(n, 1), ("far", message[1], s)))
         fill(now)
     return acts
 
 
 X, Z, Y = 0, 1, 2
 PIECES = (
-    (1, (1, 2, 1), (Y, X, Z), (False, False, True), -2.53),
-    (0, (2, 3), (X, Y, Z), (False, True, True), 1.68),
-    (0, (1, 3, 3), (Z, Y, X), (False, True, True), 2.01),
+    (1, (1, 2, 1), (Y, X, Z), (0, 0, 1), -2.53),
+    (0, (2, 3), (X, Y, Z), (0, 1, 1), 1.68),
+    (0, (1, 3, 3), (Z, Y, X), (0, 1, 1), 2.01),
 )
+GROUPS = ((4, 5), (6, 7, 8), (1, 2, 3, 0))
+RELAYED = (0, 1, 2)
 
 
 def make_streams(q_rows, k_rows):
@@ -158,14 +205,14 @@
         dict(
             peak=True,
             rows=PEAK_ROWS,
-            order=(Z, X, Y),
+            order=(X, Y, Z),
             parity=0,
-            short=(True, True, True),
+            forms=(1, 1, 1),
             offset=0.0,
         )
     ]
     used = [0, 0]
-    for kind, heights, order, short, offset in PIECES:
+    for kind, heights, order, forms, offset in PIECES:
         for n, height in enumerate(heights):
             rows = height * (q_rows // 12, k_rows // 4)[kind]
             streams.append(
@@ -176,7 +223,7 @@
                     rows=rows,
                     order=order,
                     parity=n % 2,
-                    short=short,
+                    forms=forms,
                     offset=offset,
                 )
             )
@@ -196,14 +243,16 @@
 
 
 def gramian(pair):
-    g = contract_rows(pair, pair)
+    return folded(contract_rows(pair, pair))
+
+
+def folded(g):
     return (g[:W, :W] + g[W:, W:]) + (g[:W, W:] + g[W:, :W])
 
 
 def mixer_of(gram):
-    square = jnp.dot(
-        gram, gram, precision=lax.Precision.HIGHEST, preferred_element_type=jnp.float32
-    )
+    pair = split(gram)
+    square = mixed(pair, jnp.concatenate([pair, pair], axis=0))
     mixer = split(COEFF_B * gram + COEFF_C * square)
     return jnp.concatenate([mixer, mixer], axis=0)
 
@@ -246,8 +295,8 @@
     me = tuple(lax.axis_index(name) for name in AXES)
     rows = q_rows + k_rows
 
-    def at(axis, shift):
-        there = list(me)
+    def at(axis, shift, origin=me):
+        there = list(origin)
         there[axis] = lax.rem(me[axis] + shift + sizes[axis], sizes[axis])
         return tuple(there)
 
@@ -282,26 +331,15 @@
                 for f, g in moves:
                     shifts |= {(f - g) % sizes[axis], (g - f) % sizes[axis]}
         partners += [at(axis, s) for s in sorted(shifts) if s]
+    opposite = at(0, nx // 2)
     partners += [at(3, s) for s in range(1, nh)] + [at(4, s) for s in range(1, nc)]
+    partners += [at(3, s, opposite) for s in range(1, nh)]
     barrier = pltpu.get_barrier_semaphore()
     for there in partners:
         pl.semaphore_signal(
             barrier, inc=1, device_id=there, device_id_type=pl.DeviceIdType.MESH
         )
 
-    place = me[3] * nc + me[4]
-    lane = lax.broadcasted_iota(jnp.int32, (PEAK_ROWS, W), 1)
-    token = lax.broadcasted_iota(jnp.int32, (tokens, picks), 0)
-    peaks = jnp.full((PEAK_ROWS, W), LOWEST, jnp.float32)
-    for h in range(local_heads):
-        picked = []
-        for pick, heads in ((q_pick, q_heads), (k_pick, k_heads)):
-            chosen = (token == pick[h]).astype(jnp.float32).astype(jnp.bfloat16)
-            picked.append(contract_rows(chosen, heads[:, h * W : (h + 1) * W]))
-        score = jnp.sum(picked[0] * picked[1], axis=1, keepdims=True)
-        top = jnp.max(score, axis=0, keepdims=True) * SCORE_SCALE
-        peaks = jnp.where(lane == place * local_heads + h, top, peaks)
-    bufs[0][...] = peaks
 
     shaped, slot_of, sem_of, sems, pos = [], [], {}, 0, 0
     for i, stream in enumerate(streams):
@@ -344,6 +382,22 @@
         terms(n, nth_z(n))
     pl.semaphore_wait(barrier, len(partners))
 
+    lane = lax.broadcasted_iota(jnp.int32, (PEAK_ROWS, W), 1)
+
+    def scores():
+        place = me[3] * nc + me[4]
+        token = lax.broadcasted_iota(jnp.int32, (tokens, picks), 0)
+        peaks = jnp.full((PEAK_ROWS, W), LOWEST, jnp.float32)
+        for h in range(local_heads):
+            picked = []
+            for pick, heads in ((q_pick, q_heads), (k_pick, k_heads)):
+                chosen = (token == pick[h]).astype(jnp.float32).astype(jnp.bfloat16)
+                picked.append(contract_rows(chosen, heads[:, h * W : (h + 1) * W]))
+            score = jnp.sum(picked[0] * picked[1], axis=1, keepdims=True)
+            top = jnp.max(score, axis=0, keepdims=True) * SCORE_SCALE
+            peaks = jnp.where(lane == place * local_heads + h, top, peaks)
+        bufs[0][...] = peaks
+
     def rest_of_terms():
         group = 3 if (nz - lead) % 3 == 0 else 1
 
@@ -390,16 +444,81 @@
 
     half = me[0] // (nx // 2)
     mine = blocks.at[half, me[3], me[4]]
+    spans = []
+    for members in GROUPS:
+        height = sum(streams[i]["rows"] for i in members)
+        spans.append((sum(n for _, n in spans), height))
+    gathered = sems
+    sent = 0
+
+    def gather_copy(h, y, c, g, there, send):
+        number = ((h * nh + y) * nc + c) * len(GROUPS) + g
+        part = blocks.at[h, y, c, pl.ds(*spans[g])]
+        return pltpu.make_async_remote_copy(
+            src_ref=part,
+            dst_ref=part,
+            send_sem=send_sem.at[gathered + send],
+            recv_sem=recv_sem.at[gathered + number],
+            device_id=there,
+            device_id_type=pl.DeviceIdType.MESH,
+        )
+
+    def hand_on(h, y, c, g, there):
+        nonlocal sent
+        copy = gather_copy(h, y, c, g, there, sent)
+        copy.start()
+        started.append(copy)
+        sent += 1
+
+    def to_other_cores(h, y, g):
+        for s in range(1, nc):
+            hand_on(h, y, me[4], g, at(4, s))
+
+    def arrived(h, y, c, g):
+        gather_copy(h, y, c, g, me, 0).wait_recv()
+
+    def send(message):
+        if message[0] == "sum":
+            copy = remote(*message[1:])
+            copy.start()
+            started.append(copy)
+        elif message[0] == "across":
+            hand_on(half, me[3], me[4], message[1], opposite)
+        elif message[0] == "cross":
+            hand_on(half, me[3], me[4], message[1], at(3, message[2], opposite))
+        else:
+            hand_on(
+                half if message[0] == "own" else 1 - half,
+                me[3],
+                me[4],
+                message[1],
+                at(3, message[2]),
+            )
+
+    def receive(message):
+        if message[0] == "sum":
+            remote(*message[1:]).wait_recv()
+            return
+        g = message[1]
+        if message[0] == "across":
+            h, y = 1 - half, me[3]
+        else:
+            h = half if message[0] == "own" else 1 - half
+            y = lax.rem(me[3] - message[2] + nh, nh)
+        arrived(h, y, me[4], g)
+        to_other_cores(h, y, g)
+
     started = []
     for act in acts:
         if act[0] == "rest":
+            scores()
             rest_of_terms()
         elif act[0] == "send":
-            copy = remote(*act[1:])
-            copy.start()
-            started.append(copy)
+            send(act[1])
         elif act[0] == "recv":
-            remote(*act[1:]).wait_recv()
+            receive(act[1])
+        elif act[0] == "ready":
+            to_other_cores(half, me[3], act[1])
         elif act[0] == "join":
             _, i, k, way, g = act
             landed = incoming(i, k, way, g)
@@ -425,59 +544,31 @@
                 out[span, :] = fresh
                 mine[pl.ds(stream["kind"] * q_rows + stream["at"], stream["rows"]), :] = fresh
 
-    gathered = sems
-    sent = 0
-
-    def hand_on(which, there):
-        nonlocal sent
-        h, y, c = which
-        number = (h * nh + y) * nc + c
-        copy = pltpu.make_async_remote_copy(
-            src_ref=blocks.at[h, y, c],
-            dst_ref=blocks.at[h, y, c],
-            send_sem=send_sem.at[gathered + sent],
-            recv_sem=recv_sem.at[gathered + number],
-            device_id=there,
-            device_id_type=pl.DeviceIdType.MESH,
-        )
-        copy.start()
-        started.append(copy)
-        sent += 1
-
-    def arrived(which):
-        h, y, c = which
-        number = (h * nh + y) * nc + c
-        pltpu.make_async_remote_copy(
-            src_ref=blocks.at[h, y, c],
-            dst_ref=blocks.at[h, y, c],
-            send_sem=send_sem.at[gathered],
-            recv_sem=recv_sem.at[gathered + number],
-            device_id=me,
-            device_id_type=pl.DeviceIdType.MESH,
-        ).wait_recv()
-
-    own = (half, me[3], me[4])
-    far = (1 - half, me[3], me[4])
-    hand_on(own, at(0, nx // 2))
-    for s in range(1, nh):
-        hand_on(own, at(3, s))
-    for s in range(1, nc):
-        hand_on(own, at(4, s))
-    arrived(far)
-    for s in range(1, nh):
-        hand_on(far, at(3, s))
-    for s in range(1, nc):
-        hand_on(far, at(4, s))
-    for h in (half, 1 - half):
-        for s in range(1, nh):
-            other = (h, lax.rem(me[3] - s + nh, nh), me[4])
-            arrived(other)
-            for s2 in range(1, nc):
-                hand_on(other, at(4, s2))
-    for s2 in range(1, nc):
-        for h in (half, 1 - half):
-            for s in range(nh):
-                arrived((h, lax.rem(me[3] - s + nh, nh), lax.rem(me[4] - s2 + nc, nc)))
+    count = 2 * nh * nc
+    eye = lax.broadcasted_iota(jnp.int32, (W, W), 0) == lax.broadcasted_iota(
+        jnp.int32, (W, W), 1
+    )
+    starts, grams = [], [None, None]
+    for g, (first, height) in enumerate(spans):
+        for s in range(1, nc):
+            for h in (half, 1 - half):
+                for t in range(nh):
+                    other = lax.rem(me[4] - s + nc, nc)
+                    arrived(h, lax.rem(me[3] - t + nh, nh), other, g)
+        kind = 0 if first < q_rows else 1
+        height = min(height, rows - first)
+        starts.append((kind, count * first, height))
+        for h in range(2):
+            for y in range(nh):
+                for c in range(nc):
+                    number = (h * nh + y) * nc + c
+                    part = blocks[h, y, c, first : first + height, :]
+                    span = pl.ds(count * first + number * height, height)
+                    x_full[span, :] = part
+                    pairs[span, :] = split(part)
+        share = pairs[count * first : count * (first + height), :]
+        share = contract_rows(share, share)
+        grams[kind] = share if grams[kind] is None else grams[kind] + share
 
     head = lax.rem((me[0] * nz + me[1]) * ny + me[2], nx * nz * ny // 2)
     top = jnp.full((PEAK_ROWS, W), LOWEST, jnp.float32)
@@ -488,29 +579,14 @@
     peak = jnp.max(jnp.max(top, axis=1, keepdims=True), axis=0, keepdims=True)
     shrink = jnp.sqrt(CLIP_LEVEL / jnp.maximum(peak, CLIP_LEVEL))
 
-    count = 2 * nh * nc
-    starts = (0, count * q_rows)
-    heights = (count * q_rows, count * k_rows)
-    for h in range(2):
-        for y in range(nh):
-            for c in range(nc):
-                number = (h * nh + y) * nc + c
-                block = blocks[h, y, c]
-                for kind, part in ((0, block[:q_rows]), (1, block[q_rows:rows])):
-                    height = (q_rows, k_rows)[kind]
-                    span = pl.ds(starts[kind] + number * height, height)
-                    x_full[span, :] = part
-                    pairs[span, :] = split(part)
+    bounds = ((0, count * q_rows), (count * q_rows, count * k_rows))
 
     def tile(kind):
-        return pl.ds(starts[kind], heights[kind])
-
-    eye = lax.broadcasted_iota(jnp.int32, (W, W), 0) == lax.broadcasted_iota(
-        jnp.int32, (W, W), 1
-    )
+        return pl.ds(*bounds[kind])
+
     mixers, scales = [], []
     for kind in range(2):
-        gram = gramian(pairs[tile(kind), :])
+        gram = folded(grams[kind])
         diagonal = jnp.where(eye, gram, 0.0)
         trace = jnp.sum(jnp.sum(diagonal, axis=1, keepdims=True), axis=0, keepdims=True)
         scale = 1.0 / jnp.sqrt(trace + 1.0)
@@ -537,10 +613,15 @@
     for kind, (weight, out, rank) in enumerate(
         ((q_weight, q_weight_out, QR), (k_weight, k_weight_out, KR))
     ):
-        height = (q_rows, k_rows)[kind]
         mixer = mixer_of(gramian(pairs[tile(kind), :]))
-        span = pl.ds(pl.multiple_of(starts[kind] + number * height, 8), height)
-        current = x_full[span, :]
+        current = jnp.concatenate(
+            [
+                x_full[pl.ds(pl.multiple_of(at_row + number * n, 8), n), :]
+                for which, at_row, n in starts
+                if which == kind
+            ],
+            axis=0,
+        )
         ortho = COEFF_A * current + mixed(split(current), mixer)
         out[...] = (weight[...] * keep - STEP_SIZE * 0.2 * math.sqrt(rank) * ortho) * shrink
     for copy in started:
@@ -549,7 +630,7 @@
 
 def step(sizes, q_rows, k_rows, picks, tokens, local_heads):
     streams = make_streams(q_rows, k_rows)
-    acts = plan(streams, sizes)
+    acts = plan(streams, GROUPS, sizes)
     rows = q_rows + k_rows
     width = sizes[0] * sizes[1] * sizes[2] // 2 * W
     count = 2 * sizes[3] * sizes[4]
@@ -573,8 +654,8 @@
             bufs.append(pltpu.VMEM(source + tile, jnp.float32))
             bufs.append(pltpu.VMEM((max(n[k] - 1, 1),) + lead[k] + tile, jnp.float32))
     scratch += [
-        pltpu.SemaphoreType.DMA((messages + count,)),
-        pltpu.SemaphoreType.DMA((messages + count,)),
+        pltpu.SemaphoreType.DMA((messages + count * len(GROUPS),)),
+        pltpu.SemaphoreType.DMA((messages + count * len(GROUPS),)),
     ]
     vmem = pl.BlockSpec(memory_space=pltpu.VMEM)
     hbm = pl.BlockSpec(memory_space=pltpu.HBM)

time: 87.2 us -> 85.2 us (0.977)
  Pallas kernels: 86.4 us -> 84.4 us
    pallas_call x1, Pallas kernels: 85.8 us -> 83.7 us  [local(): step(sizes, q_rows, k_rows, picks, tokens, local_heads)]
where the time goes in v4:
time: 85.2 us; the launch traced here: 85 us
  Pallas kernels  84.4 us (99%)
    pallas_call x1, Pallas kernels, local(): step(sizes, q_rows, k_rows, picks, tokens, local_heads)  83.7 us

profile of v4, /device:TPU:1, one launch (start us, length us, event | category | flops | bytes accessed | tf_op | source)
XLA Modules:
  0.0 85.0 jit_solution(7629824596019817540)
XLA Ops:
  0.6 83.7 %muon_clip.1 = (f32[96,128]{1,0:T(8,128)S(1)}, f32[32,128]{1,0:T(8,128)S(1)}, f32[96,128]{1,0:T(8,128)S(1)}, f32[32,128]{1,0:T(8,128)S(1)}) custom-call(bf16[192,256]{1,0:T(8,128)(2,1)} %bitcast.16, bf16[64,256]{1,0:T(8,128)(2,1)} %bitcast.19, bf16[256,6144]{1,0:T(8,128)(2,1)} %q_grad_hbm.1, bf16[256,6144]{1,0:T(8,128)(2,1)} %k_grad_hbm.1, ...), custom_call_target="tpu_custom_call" | custom-call | tf_op jit(solution)/shard_map/muon_clip/pallas_call | solution.py:717
  84.4 0.7 hand_out.1
